TPU v7x, 32 devices: a whole 2x2x4 slice. The times are simulated.
32 devices in a mesh: dp: 8 (over z, y), group: 4 (over x, core).
Axes of the slice: x: 2, y: 2, z: 4, core: 2. Of those that a mesh axis runs over, the one named last changes fastest.
Arguments:
- features: bfloat16 [4096, 512], P(('dp', 'group')), may hold values from -6 to 6
- head_weight: bfloat16 [512, 512], replicated, may hold values from -0.25 to 0.25
- owner_of_image: int32 [4096, 1], P(('dp', 'group')), may hold values from 0 to 7; in each aligned block of 128 rows (0 to 127, 128 to 255, ...) at most 32 rows name the same one
- class_slot: int32 [4096], P(('dp', 'group')), may hold values from 0 to 49
- is_query: int32 [4096], P(('dp', 'group')), may hold values 0 or 1
- episode_ways: int32 [32], P(('dp', 'group')), may hold values from 5 to 50
Outputs:
- grad_features: bfloat16 [4096, 512], P(('dp', 'group'))
- grad_weight: float32 [512, 512], replicated
- losses: float32 [32], P(('dp', 'group'))
Inputs may be any that keep to these rules, and one draw needn't show every extreme that they name: `owner_of_image`: among the rows of one device at most 32 name any one owner, a bound that some block reaches.
All inputs are finite; a program needn't handle non-finite values. No bound on the sum of `is_query` on one device may be relied on, other than what follows from the above.
Results may differ from a plain program's by a relative error of at most 0.0037.
The roundings to bfloat16 on the way count: a program that leaves them out, or rounds other values in their place, can miss the bound.
Values may be sent and summed in bfloat16 or wider, within the bound.
No kernel may reach another device: no remote copies, remote signals or barrier semaphores. Data moves between devices by JAX's collectives and lax.ppermute only.
A program may use at most 64 MiB of HBM per device.

v0:
```python
import functools

import jax
import jax.numpy as jnp
from jax import lax
from jax.experimental import pallas as pl
from jax.experimental.pallas import tpu as pltpu
from jax.sharding import PartitionSpec as P


D = 512
WAYS_MAX = 50
CODE_ROWS = 8


def episode_losses(embeds, codes, ways_table):
    count_ep = ways_table.shape[0]
    is_live = codes > 0
    code_value = jnp.maximum(codes - 1, 0)
    query_rows = is_live & (code_value % 2 == 1)
    support_rows = is_live & (code_value % 2 == 0)
    slot_value = code_value // 2
    episode = slot_value // WAYS_MAX
    raw_class = slot_value % WAYS_MAX
    episode_hot = episode[:, None] == jnp.arange(count_ep, dtype=jnp.int32)[None, :]
    row_ways = jnp.sum(jnp.where(episode_hot, ways_table[None, :], 0), axis=1)
    label_id = episode * WAYS_MAX + raw_class % row_ways
    classes = jnp.arange(count_ep * WAYS_MAX, dtype=jnp.int32)
    class_hot = label_id[:, None] == classes[None, :]
    support_hot = (class_hot & support_rows[:, None]).astype(jnp.float32)
    counts = jnp.sum(support_hot, axis=0)
    class_sums = jnp.dot(support_hot.T, embeds, precision=lax.Precision.HIGHEST)
    prototypes = class_sums / jnp.maximum(counts, 1.0)[:, None]
    class_ways = jnp.repeat(ways_table, WAYS_MAX)
    class_valid = classes % WAYS_MAX < class_ways
    allowed = (episode[:, None] == (classes // WAYS_MAX)[None, :]) & class_valid[None, :]
    cross_term = jnp.dot(embeds, prototypes.T, precision=lax.Precision.HIGHEST)
    distance = (
        jnp.sum(embeds * embeds, axis=1)[:, None]
        - 2.0 * cross_term
        + jnp.sum(prototypes * prototypes, axis=1)[None, :]
    )
    scores = -distance * D ** (-0.5)
    masked = jnp.where(allowed, scores, -1e30)
    row_max = jnp.max(masked, axis=1, keepdims=True)
    log_total = row_max[:, 0] + jnp.log(jnp.sum(jnp.exp(masked - row_max), axis=1))
    picked = jnp.sum(jnp.where(class_hot, scores, 0.0), axis=1)
    per_query = jnp.where(query_rows, log_total - picked, 0.0)
    hot_float = episode_hot.astype(jnp.float32)
    query_count = jnp.sum(hot_float * query_rows[:, None].astype(jnp.float32), axis=0)
    return jnp.sum(hot_float * per_query[:, None], axis=0) / jnp.maximum(query_count, 1.0)


def times_transpose(left, right):
    return lax.dot_general(
        left, right, (((1,), (1,)), ((), ())), preferred_element_type=jnp.float32
    )


def inner_rows(left, right):
    return lax.dot_general(
        left, right, (((0,), (0,)), ((), ())), preferred_element_type=jnp.float32
    )


def routed(features, head_weight, owner_of_image, class_slot, is_query, episode_ways):
    peers = lax.axis_size("dp")
    row_count = features.shape[0]
    capacity = 2 * row_count // peers
    target = owner_of_image[:, 0]
    one_hot = (target[:, None] == jnp.arange(peers, dtype=jnp.int32)[None, :]).astype(jnp.int32)
    before = jnp.cumsum(one_hot, axis=0) - one_hot
    position = jnp.sum(one_hot * before, axis=1)
    flat_slot = target * capacity + position
    codes = class_slot * 2 + is_query + 1
    send_rows = (
        jnp.zeros((peers * capacity, D), jnp.bfloat16)
        .at[flat_slot]
        .set(features)
        .reshape(peers, capacity, D)
    )
    send_codes = (
        jnp.zeros((peers * capacity,), jnp.int32).at[flat_slot].set(codes).reshape(peers, capacity)
    )
    got_rows, got_codes = (
        lax.all_to_all(send_rows, "dp", split_axis=0, concat_axis=0, tiled=True),
        lax.all_to_all(send_codes, "dp", split_axis=0, concat_axis=0, tiled=True),
    )
    got_rows = got_rows.reshape(peers * capacity, D)
    got_codes = got_codes.reshape(peers * capacity)
    got_embeds = jnp.dot(got_rows, head_weight, preferred_element_type=jnp.float32).astype(
        jnp.bfloat16
    )
    losses, pull = jax.vjp(
        lambda e: episode_losses(e, got_codes, episode_ways), got_embeds.astype(jnp.float32)
    )
    grad_embeds = pull(jnp.ones_like(losses))[0].astype(jnp.bfloat16)
    partial_value = inner_rows(got_rows, grad_embeds)
    outgoing = times_transpose(grad_embeds, head_weight).astype(jnp.bfloat16)
    returned = lax.all_to_all(
        outgoing.reshape(peers, capacity, D), "dp", split_axis=0, concat_axis=0, tiled=True
    )
    own_rows = returned.reshape(peers * capacity, D)[flat_slot]
    grad_weight = lax.psum(partial_value, ("dp", "group"))
    return (own_rows, grad_weight, losses)


def pack_kernel(features, owner, slot, query, ways, block, ints, sems):
    rows = features.shape[0]
    copies = [pltpu.make_async_copy(features, block.at[:rows, :], sems.at[0])]
    for k, source in enumerate((owner, slot, query)):
        copies.append(pltpu.make_async_copy(source, ints.at[k], sems.at[k + 1]))
    for copy in copies:
        copy.start()
    block[rows:, :] = jnp.zeros((CODE_ROWS, D), jnp.bfloat16)
    for copy in copies[1:]:
        copy.wait()
    line = lax.broadcasted_iota(jnp.int32, (CODE_ROWS, rows), 0)
    fields = jnp.where(
        line == 0,
        ints[0],
        jnp.where(line == 1, ints[1], jnp.where(line == 2, ints[2], ways[...])),
    )
    block[rows:, :rows] = fields.astype(jnp.float32).astype(jnp.bfloat16)
    copies[0].wait()


def embed_kernel(count, step, block, weight, *refs):
    embeds, turned, codes = refs[-3:]
    rows = block.shape[0] - CODE_ROWS
    device = ring_device(count, step)
    start = pl.multiple_of(device * rows, rows)
    values = dot(block[:rows, :], weight[...]).astype(jnp.bfloat16)
    embeds[pl.ds(start, rows), :] = values
    turned[:, pl.ds(start, rows)] = block[:rows, :].T
    wide = values.astype(jnp.float32)
    squares = jnp.sum(wide * wide, axis=1, keepdims=True)
    lengths = jnp.broadcast_to(squares, (rows, 128)).T[:CODE_ROWS, :rows]
    line = lax.broadcasted_iota(jnp.int32, (CODE_ROWS, rows), 0)
    codes[:, pl.ds(start, rows)] = jnp.where(
        line == 4, lengths, block[rows:, :rows].astype(jnp.float32)
    )


def split(value):
    high = value.astype(jnp.bfloat16)
    return high, (value - high.astype(jnp.float32)).astype(jnp.bfloat16)


def dot(left, right, on=(1, 0)):
    return lax.dot_general(
        left, right, (((on[0],), (on[1],)), ((), ())), preferred_element_type=jnp.float32
    )


def ring_order(count):
    return [d for d in range(0, count, 2)] + [d for d in range(count - 1, 0, -1) if d % 2]


def ring_steps(count):
    steps = [0]
    for k in range(1, count // 2 + 1):
        steps.append(-k)
        if k <= (count - 1) // 2:
            steps.append(k)
    return steps


def ring_device(count, step):
    me = lax.axis_index("dp")
    spot = jnp.where(me % 2 == 0, me // 2, count - 1 - me // 2)
    at = lax.rem(spot + (step + count), count)
    return jnp.where(2 * at < count, 2 * at, 2 * (count - 1 - at) + 1)


def main_kernel(count, embeds, turned, codes, give, grads, loss, hot_s, g_high, g_low):
    total = embeds.shape[0]
    rows = total // count
    classes = count * WAYS_MAX
    scale = D ** (-0.5)
    me = lax.axis_index("dp")
    step = min(total, 256)
    parts = [slice(at, at + step) for at in range(0, total, step)]

    owner, slot, query = codes[0:1, :], codes[1:2, :], codes[2:3, :]
    ways = jnp.zeros_like(owner)
    queries = jnp.zeros_like(owner)
    for p in range(count):
        mine = owner == float(p)
        ways = jnp.where(mine, codes[3:4, p * rows : p * rows + 1], ways)
        total_q = jnp.sum(jnp.where(mine, query, 0.0), axis=1, keepdims=True)
        queries = jnp.where(mine, total_q, queries)
    share = query / jnp.maximum(queries, 1.0)
    label = slot - jnp.floor((slot + 0.5) / ways) * ways
    first = (owner * float(WAYS_MAX)).astype(jnp.int32)
    last = first + ways.astype(jnp.int32)
    own_class = first + label.astype(jnp.int32)
    support_class = jnp.where(query > 0.5, -1, own_class)

    ids = lax.broadcasted_iota(jnp.int32, (classes, total), 0)
    hot_value = jnp.where(ids == support_class, 1.0, 0.0)
    counts = jnp.maximum(jnp.sum(hot_value, axis=1, keepdims=True), 1.0)
    hot_s[...] = hot_value.astype(jnp.bfloat16)
    protos = dot(hot_s[...], embeds[...]) / counts
    p_high, p_low = split(protos)
    p_length = jnp.sum(protos * protos, axis=1, keepdims=True)

    g_sum = jnp.zeros((classes, 1), jnp.float32)
    loss_sum = jnp.zeros((1, 1), jnp.float32)
    row_sums = []
    for part in parts:
        e = embeds[part, :]
        product = dot(p_high, e, (1, 1)) + dot(p_low, e, (1, 1))
        scores = -(codes[4:5, part] - 2.0 * product + p_length) * scale
        c = lax.broadcasted_iota(jnp.int32, (classes, step), 0)
        masked = jnp.where((c >= first[:, part]) & (c < last[:, part]), scores, -1e30)
        top = jnp.max(masked, axis=0, keepdims=True)
        powers = jnp.exp(masked - top)
        norm = jnp.sum(powers, axis=0, keepdims=True)
        is_own = c == own_class[:, part]
        picked = jnp.sum(jnp.where(is_own, scores, 0.0), axis=0, keepdims=True)
        mine = owner[:, part] == me.astype(jnp.float32)
        losses = share[:, part] * (top + jnp.log(norm) - picked)
        loss_sum += jnp.sum(jnp.where(mine, losses, 0.0), axis=1, keepdims=True)
        g = (powers * (1.0 / norm) - jnp.where(is_own, 1.0, 0.0)) * (
            share[:, part] * (2.0 * scale)
        )
        g_sum += jnp.sum(g, axis=1, keepdims=True)
        row_sums.append(jnp.sum(g, axis=0, keepdims=True))
        high, low = split(g)
        g_high[:, part] = high
        g_low[:, part] = low
    loss[...] = jnp.broadcast_to(loss_sum, loss.shape)

    e = embeds[...]
    d_protos = dot(g_high[...], e) + dot(g_low[...], e) - g_sum * protos
    s_high = (d_protos / counts).astype(jnp.bfloat16)
    for part, row_sum in zip(parts, row_sums):
        value = (
            dot(g_high[:, part], p_high, (0, 0))
            + dot(g_low[:, part], p_high, (0, 0))
            + dot(g_high[:, part], p_low, (0, 0))
            + dot(hot_s[:, part], s_high, (0, 0))
        )
        back = jnp.broadcast_to(row_sum, (128, step)).T[:, :1]
        value = value - back * embeds[part, :].astype(jnp.float32)
        grads[part, :] = value.astype(jnp.bfloat16)

    half = D // 2
    other = 1 - lax.axis_index("group") % 2
    give_at = pl.multiple_of(other * half, half)
    give[...] = dot(turned[pl.ds(give_at, half), :], grads[...]).astype(give.dtype)


def rest_kernel(turned, grads, weight, keep, grad_rows):
    rows, half = grad_rows.shape[0], keep.shape[0]
    keep_at = pl.multiple_of(lax.axis_index("group") % 2 * half, half)
    keep[...] = dot(turned[pl.ds(keep_at, half), :], grads[...])
    own = grads[pl.ds(pl.multiple_of(lax.axis_index("dp") * rows, rows), rows), :]
    grad_rows[...] = dot(own, weight[...], (1, 1)).astype(jnp.bfloat16)


def loss_kernel(value, loss):
    loss[...] = value[:1, :1]


def vmem(n):
    return [pl.BlockSpec(memory_space=pltpu.VMEM)] * n


def gathered(features, head_weight, owner_of_image, class_slot, is_query, episode_ways):
    count = lax.axis_size("dp")
    groups = lax.axis_size("group")
    rows = features.shape[0]
    classes = count * WAYS_MAX
    total = rows * count

    order = ring_order(count)
    ahead = [(order[i], order[(i + 1) % count]) for i in range(count)]
    behind = [(b, a) for a, b in ahead]

    hbm = pl.BlockSpec(memory_space=pltpu.HBM)
    block = pl.pallas_call(
        pack_kernel,
        out_shape=jax.ShapeDtypeStruct((rows + CODE_ROWS, D), jnp.bfloat16),
        in_specs=[hbm] * 4 + vmem(1),
        out_specs=vmem(1)[0],
        scratch_shapes=[
            pltpu.VMEM((3, 1, rows), jnp.int32),
            pltpu.SemaphoreType.DMA((4,)),
        ],
        compiler_params=pltpu.CompilerParams(vmem_limit_bytes=4 * 2**20),
        name="pack",
    )(
        *(
            pltpu.with_memory_space_constraint(value, pltpu.HBM)
            for value in (
                features,
                owner_of_image.reshape(1, rows),
                class_slot.reshape(1, rows),
                is_query.reshape(1, rows),
            )
        ),
        episode_ways.reshape(1, 1),
    )

    blocks = [block]
    fore = back = block
    for k in range(1, count // 2 + 1):
        fore = lax.ppermute(fore, "dp", ahead)
        blocks.append(fore)
        if k <= (count - 1) // 2:
            back = lax.ppermute(back, "dp", behind)
            blocks.append(back)

    held = (
        jax.ShapeDtypeStruct((total, D), jnp.bfloat16),
        jax.ShapeDtypeStruct((D, total), jnp.bfloat16),
        jax.ShapeDtypeStruct((CODE_ROWS, total), jnp.float32),
    )
    state = ()
    for step, value in zip(ring_steps(count), blocks):
        state = pl.pallas_call(
            functools.partial(embed_kernel, count, step),
            out_shape=held,
            in_specs=vmem(2 + len(state)),
            out_specs=tuple(vmem(3)),
            input_output_aliases={2 + i: i for i in range(len(state))},
            cost_estimate=pl.CostEstimate(
                flops=16 * 2 * rows * D * D, bytes_accessed=0, transcendentals=0
            ),
            compiler_params=pltpu.CompilerParams(vmem_limit_bytes=8 * 2**20),
            name="embed",
        )(value, head_weight, *state)

    give, grads, loss = pl.pallas_call(
        functools.partial(main_kernel, count),
        out_shape=(
            pltpu.VMEM((D // 2, D), jnp.bfloat16),
            pltpu.VMEM((total, D), jnp.bfloat16),
            pltpu.VMEM((8, 128), jnp.float32),
        ),
        in_specs=vmem(3),
        out_specs=tuple(vmem(3)),
        scratch_shapes=[pltpu.VMEM((classes, total), jnp.bfloat16)] * 3,
        compiler_params=pltpu.CompilerParams(vmem_limit_bytes=32 * 2**20),
        name="episodes",
    )(*state)
    keep, grad_rows = pl.pallas_call(
        rest_kernel,
        out_shape=(
            pltpu.VMEM((D // 2, D), jnp.float32),
            pltpu.VMEM((rows, D), jnp.bfloat16),
        ),
        in_specs=vmem(3),
        out_specs=tuple(vmem(2)),
        cost_estimate=pl.CostEstimate(flops=2**32, bytes_accessed=0, transcendentals=0),
        compiler_params=pltpu.CompilerParams(vmem_limit_bytes=8 * 2**20),
        name="rest",
    )(state[1], grads, head_weight)

    loss = pl.pallas_call(
        loss_kernel,
        out_shape=jax.ShapeDtypeStruct((1, 1), jnp.float32),
        in_specs=vmem(1),
        out_specs=vmem(1)[0],
        cost_estimate=pl.CostEstimate(flops=2**28, bytes_accessed=0, transcendentals=0),
        compiler_params=pltpu.CompilerParams(vmem_limit_bytes=2**20),
        name="loss",
    )(loss)

    pairs = [(i, i ^ 1) for i in range(groups)]
    half = keep + lax.ppermute(give, "group", pairs).astype(jnp.float32)
    terms = [half]
    move = 2
    while move < groups:
        half = sum(terms[1:], terms[0].astype(jnp.float32))
        sent = half.astype(jnp.bfloat16)
        got = lax.ppermute(sent, "group", [(i, i ^ move) for i in range(groups)])
        terms = [sent, got]
        move *= 2
    others = [lax.ppermute(t, "group", pairs) for t in terms]
    half = sum(terms[1:], terms[0].astype(jnp.float32))
    other = sum(others[1:], others[0].astype(jnp.float32))
    bit = lax.axis_index("group") % 2
    low = jnp.where(bit == 0, half, other)
    high = jnp.where(bit == 0, other, half)
    return grad_rows, jnp.concatenate([low, high]), loss.reshape(1)


def solution(mesh):
    in_specs = (
        P(("dp", "group"), None),
        P(),
        P(("dp", "group"), None),
        P(("dp", "group")),
        P(("dp", "group")),
        P(("dp", "group")),
    )
    out_specs = (P(("dp", "group"), None), P(), P(("dp", "group")))

    def on_device(features, head_weight, owner_of_image, class_slot, is_query, episode_ways):
        count, groups = lax.axis_size("dp"), lax.axis_size("group")
        fits = (
            2 <= count <= 8
            and groups > 1
            and groups & (groups - 1) == 0
            and features.shape[0] == 128
            and episode_ways.shape[0] == 1
        )
        run = gathered if fits else routed
        return run(
            features, head_weight, owner_of_image, class_slot, is_query, episode_ways
        )

    return jax.shard_map(
        on_device, mesh=mesh, in_specs=in_specs, out_specs=out_specs, check_vma=False
    )
```

profile of v0, /device:TPU:0, one launch (start us, length us, event | category | flops | bytes accessed | tf_op | source)
XLA Modules:
  0.0 44.3 jit_solution(15908877695529175708)
XLA Ops:
  1.3 0.9 %pack.1.block = bf16[136,512]{1,0:T(8,128)(2,1)S(1)} custom-call(bf16[128,512]{1,0:T(8,128)(2,1)} %features.1, s32[1,128]{1,0:T(1,128)} %bitcast.6, s32[1,128]{1,0:T(1,128)} %bitcast.7, s32[1,128]{1,0:T(1,128)} %bitcast.8, s32[1,1]{1,0:T(1,128)} %bitcast.5.ways), custom_call_target="tpu_custom_call" | custom-call | tf_op jit(solution)/shard_map/pack/pallas_call | solution.py:283
  2.2 3.1 %collective-permute-start = (bf16[136,512]{1,0:T(8,128)(2,1)S(1)}, bf16[136,512]{1,0:T(8,128)(2,1)S(1)}, u32[]{:S(2)}, u32[]{:S(2)}) collective-permute-start(bf16[136,512]{1,0:T(8,128)(2,1)S(1)} %pack.1.block), channel_id=1, source_target_pairs={{0,8},{8,16},{16,24},{24,28},{28,20},{20,12},{12,4},{4,0},{1,9},{9... | collective-permute-start | bytes 417800 | tf_op jit(solution)/shard_map/ppermute | solution.py:310
  5.3 1.0 %copy-done = bf16[512,512]{1,0:T(8,128)(2,1)S(1)} copy-done((bf16[512,512]{1,0:T(8,128)(2,1)S(1)}, bf16[512,512]{1,0:T(8,128)(2,1)}, u32[]{:S(2)}) %copy-start) | copy-done | bytes 524312
  6.4 0.4 embed.8
  6.8 2.2 %collective-permute-done.block = bf16[136,512]{1,0:T(8,128)(2,1)S(1)} collective-permute-done((bf16[136,512]{1,0:T(8,128)(2,1)S(1)}, bf16[136,512]{1,0:T(8,128)(2,1)S(1)}, u32[]{:S(2)}, u32[]{:S(2)}) %collective-permute-start) | collective-permute-done | bytes 139296 | tf_op jit(solution)/shard_map/ppermute | solution.py:310
  8.9 1.8 %collective-permute-start.1 = (bf16[136,512]{1,0:T(8,128)(2,1)S(1)}, bf16[136,512]{1,0:T(8,128)(2,1)S(1)}, u32[]{:S(2)}, u32[]{:S(2)}) collective-permute-start(bf16[136,512]{1,0:T(8,128)(2,1)S(1)} %collective-permute-done.block), channel_id=1, source_target_pairs={{0,8},{8,16},{16,24},{24,28},{28,20},{20,12},{12,4},{4,0},{1,9},{9... | collective-permute-start | bytes 417800 | tf_op jit(solution)/shard_map/ppermute | solution.py:310
  10.7 0.2 collective-permute-start.5
  11.0 0.4 embed.9
  11.4 0.4 embed.10
  11.7 2.3 %collective-permute-done.1.block = bf16[136,512]{1,0:T(8,128)(2,1)S(1)} collective-permute-done((bf16[136,512]{1,0:T(8,128)(2,1)S(1)}, bf16[136,512]{1,0:T(8,128)(2,1)S(1)}, u32[]{:S(2)}, u32[]{:S(2)}) %collective-permute-start.1) | collective-permute-done | bytes 139296 | tf_op jit(solution)/shard_map/ppermute | solution.py:310
  14.0 1.8 %collective-permute-start.2 = (bf16[136,512]{1,0:T(8,128)(2,1)S(1)}, bf16[136,512]{1,0:T(8,128)(2,1)S(1)}, u32[]{:S(2)}, u32[]{:S(2)}) collective-permute-start(bf16[136,512]{1,0:T(8,128)(2,1)S(1)} %collective-permute-done.1.block), channel_id=1, source_target_pairs={{0,8},{8,16},{16,24},{24,28},{28,20},{20,12},{12,4},{4,0},{1,9},{9... | collective-permute-start | bytes 417800 | tf_op jit(solution)/shard_map/ppermute | solution.py:310
  15.8 0.2 collective-permute-start.6
  16.0 0.4 embed.11
  16.4 0.4 embed.12
  16.8 2.7 %collective-permute-done.2.block = bf16[136,512]{1,0:T(8,128)(2,1)S(1)} collective-permute-done((bf16[136,512]{1,0:T(8,128)(2,1)S(1)}, bf16[136,512]{1,0:T(8,128)(2,1)S(1)}, u32[]{:S(2)}, u32[]{:S(2)}) %collective-permute-start.2) | collective-permute-done | bytes 139296 | tf_op jit(solution)/shard_map/ppermute | solution.py:310
  19.5 2.1 %collective-permute-start.3 = (bf16[136,512]{1,0:T(8,128)(2,1)S(1)}, bf16[136,512]{1,0:T(8,128)(2,1)S(1)}, u32[]{:S(2)}, u32[]{:S(2)}) collective-permute-start(bf16[136,512]{1,0:T(8,128)(2,1)S(1)} %collective-permute-done.2.block), channel_id=1, source_target_pairs={{0,8},{8,16},{16,24},{24,28},{28,20},{20,12},{12,4},{4,0},{1,9},{9... | collective-permute-start | bytes 417800 | tf_op jit(solution)/shard_map/ppermute | solution.py:310
  21.6 0.4 embed.13
  22.0 0.4 embed.14
  22.4 2.2 %collective-permute-done.3.block = bf16[136,512]{1,0:T(8,128)(2,1)S(1)} collective-permute-done((bf16[136,512]{1,0:T(8,128)(2,1)S(1)}, bf16[136,512]{1,0:T(8,128)(2,1)S(1)}, u32[]{:S(2)}, u32[]{:S(2)}) %collective-permute-start.3) | collective-permute-done | bytes 139296 | tf_op jit(solution)/shard_map/ppermute | solution.py:310
  24.6 0.4 embed.15
  24.9 6.3 %episodes.1 = (bf16[256,512]{1,0:T(8,128)(2,1)S(1)}, bf16[1024,512]{1,0:T(8,128)(2,1)S(1)}, f32[8,128]{1,0:T(8,128)S(1)}) custom-call(bf16[1024,512]{1,0:T(8,128)(2,1)S(1)} %get-tuple-element.54.embeds, bf16[512,1024]{1,0:T(8,128)(2,1)S(1)} %get-tuple-element.53.turned, f32[8,1024]{1,0:T(8,128)S(1)} %get-tuple-element.55.codes), custom_call_target="tpu_custom_call" | custom-call | tf_op jit(solution)/shard_map/episodes/pallas_call | solution.py:336
  31.2 0.1 collective-permute-start.7
  31.3 0.5 %rest.1 = (f32[256,512]{1,0:T(8,128)S(1)}, bf16[128,512]{1,0:T(8,128)(2,1)S(1)}) custom-call(bf16[512,1024]{1,0:T(8,128)(2,1)S(1)} %get-tuple-element.53.turned, bf16[1024,512]{1,0:T(8,128)(2,1)S(1)} %get-tuple-element.56.grads, bf16[512,512]{1,0:T(8,128)(2,1)S(1)} %copy-done.1), custom_call_target="tpu_custom_call" | custom-call | flops 4294967296 | tf_op jit(solution)/shard_map/rest/pallas_call | solution.py:349
  31.9 1.0 %collective-permute-done.7 = bf16[256,512]{1,0:T(8,128)(2,1)S(1)} collective-permute-done((bf16[256,512]{1,0:T(8,128)(2,1)S(1)}, bf16[256,512]{1,0:T(8,128)(2,1)S(1)}, u32[]{:S(2)}, u32[]{:S(2)}) %collective-permute-start.7) | collective-permute-done | bytes 262176 | tf_op jit(solution)/shard_map/ppermute | solution.py:373
  32.8 0.1 add_convert_fusion
  32.9 2.1 %collective-permute-start.8 = (bf16[256,512]{1,0:T(8,128)(2,1)S(1)}, bf16[256,512]{1,0:T(8,128)(2,1)S(1)}, u32[]{:S(2)}, u32[]{:S(2)}) collective-permute-start(bf16[256,512]{1,0:T(8,128)(2,1)S(1)} %add_convert_fusion), channel_id=1, source_target_pairs={{0,2},{1,3},{2,0},{3,1},{4,6},{5,7},{6,4},{7,5},{8,10},{9,11},{10,... | collective-permute-start | bytes 786440 | tf_op jit(solution)/shard_map/ppermute | solution.py:379
  35.0 6.6 %collective-permute-done.8 = bf16[256,512]{1,0:T(8,128)(2,1)S(1)} collective-permute-done((bf16[256,512]{1,0:T(8,128)(2,1)S(1)}, bf16[256,512]{1,0:T(8,128)(2,1)S(1)}, u32[]{:S(2)}, u32[]{:S(2)}) %collective-permute-start.8) | collective-permute-done | bytes 262176 | tf_op jit(solution)/shard_map/ppermute | solution.py:379
  41.6 0.7 %copy.51 = bf16[128,512]{1,0:T(8,128)(2,1)} copy(bf16[128,512]{1,0:T(8,128)(2,1)S(1)} %get-tuple-element.63) | data formatting | bytes 262144
  42.2 0.5 %loss.1 = f32[1,1]{1,0:T(1,128)} custom-call(f32[8,128]{1,0:T(8,128)S(1)} %get-tuple-element.60.value), custom_call_target="tpu_custom_call" | custom-call | flops 268435456 | tf_op jit(solution)/shard_map/loss/pallas_call | solution.py:362
  42.7 0.4 collective-permute-done.10
  43.1 0.2 fusion.1
  43.3 1.0 %pad_maximum_fusion = f32[512,512]{1,0:T(8,128)} fusion(f32[256,512]{1,0:T(8,128)S(1)} %get-tuple-element.62, f32[256,512]{1,0:T(8,128)S(1)} %get-tuple-element.61), kind=kLoop, calls=%fused_computation | loop fusion | flops 262144 | bytes 2097152 | tf_op jit(solution)/shard_map/concatenate | solution.py:388
  (10 shorter events, 0.0 us)
Async XLA Ops:
  2.2 6.7 %collective-permute-start = (bf16[136,512]{1,0:T(8,128)(2,1)S(1)}, bf16[136,512]{1,0:T(8,128)(2,1)S(1)}, u32[]{:S(2)}, u32[]{:S(2)}) collective-permute-start(bf16[136,512]{1,0:T(8,128)(2,1)S(1)} %pack.1.block), channel_id=1, source_target_pairs={{0,8},{8,16},{16,24},{24,28},{28,20},{20,12},{12,4},{4,0},{1,9},{9... | collective-permute-start | bytes 417800 | tf_op jit(solution)/shard_map/ppermute | solution.py:310
  5.3 5.4 %collective-permute-start.4 = (bf16[136,512]{1,0:T(8,128)(2,1)S(1)}, bf16[136,512]{1,0:T(8,128)(2,1)S(1)}, u32[]{:S(2)}, u32[]{:S(2)}) collective-permute-start(bf16[136,512]{1,0:T(8,128)(2,1)S(1)} %pack.1.block), channel_id=1, source_target_pairs={{8,0},{16,8},{24,16},{28,24},{20,28},{12,20},{4,12},{0,4},{9,1},{1... | collective-permute-start | bytes 417800 | tf_op jit(solution)/shard_map/ppermute | solution.py:313
  5.3 1.0 %copy-start = (bf16[512,512]{1,0:T(8,128)(2,1)S(1)}, bf16[512,512]{1,0:T(8,128)(2,1)}, u32[]{:S(2)}) copy-start(bf16[512,512]{1,0:T(8,128)(2,1)} %weight.17) | copy-start | bytes 1572868
  8.9 5.1 %collective-permute-start.1 = (bf16[136,512]{1,0:T(8,128)(2,1)S(1)}, bf16[136,512]{1,0:T(8,128)(2,1)S(1)}, u32[]{:S(2)}, u32[]{:S(2)}) collective-permute-start(bf16[136,512]{1,0:T(8,128)(2,1)S(1)} %collective-permute-done.block), channel_id=1, source_target_pairs={{0,8},{8,16},{16,24},{24,28},{28,20},{20,12},{12,4},{4,0},{1,9},{9... | collective-permute-start | bytes 417800 | tf_op jit(solution)/shard_map/ppermute | solution.py:310
  10.7 5.1 %collective-permute-start.5 = (bf16[136,512]{1,0:T(8,128)(2,1)S(1)}, bf16[136,512]{1,0:T(8,128)(2,1)S(1)}, u32[]{:S(2)}, u32[]{:S(2)}) collective-permute-start(bf16[136,512]{1,0:T(8,128)(2,1)S(1)} %collective-permute-done.4.block), channel_id=1, source_target_pairs={{8,0},{16,8},{24,16},{28,24},{20,28},{12,20},{4,12},{0,4},{9,1},{1... | collective-permute-start | bytes 417800 | tf_op jit(solution)/shard_map/ppermute | solution.py:313
  14.0 5.5 %collective-permute-start.2 = (bf16[136,512]{1,0:T(8,128)(2,1)S(1)}, bf16[136,512]{1,0:T(8,128)(2,1)S(1)}, u32[]{:S(2)}, u32[]{:S(2)}) collective-permute-start(bf16[136,512]{1,0:T(8,128)(2,1)S(1)} %collective-permute-done.1.block), channel_id=1, source_target_pairs={{0,8},{8,16},{16,24},{24,28},{28,20},{20,12},{12,4},{4,0},{1,9},{9... | collective-permute-start | bytes 417800 | tf_op jit(solution)/shard_map/ppermute | solution.py:310
  15.8 6.2 %collective-permute-start.6 = (bf16[136,512]{1,0:T(8,128)(2,1)S(1)}, bf16[136,512]{1,0:T(8,128)(2,1)S(1)}, u32[]{:S(2)}, u32[]{:S(2)}) collective-permute-start(bf16[136,512]{1,0:T(8,128)(2,1)S(1)} %collective-permute-done.5.block), channel_id=1, source_target_pairs={{8,0},{16,8},{24,16},{28,24},{20,28},{12,20},{4,12},{0,4},{9,1},{1... | collective-permute-start | bytes 417800 | tf_op jit(solution)/shard_map/ppermute | solution.py:313
  19.5 5.1 %collective-permute-start.3 = (bf16[136,512]{1,0:T(8,128)(2,1)S(1)}, bf16[136,512]{1,0:T(8,128)(2,1)S(1)}, u32[]{:S(2)}, u32[]{:S(2)}) collective-permute-start(bf16[136,512]{1,0:T(8,128)(2,1)S(1)} %collective-permute-done.2.block), channel_id=1, source_target_pairs={{0,8},{8,16},{16,24},{24,28},{28,20},{20,12},{12,4},{4,0},{1,9},{9... | collective-permute-start | bytes 417800 | tf_op jit(solution)/shard_map/ppermute | solution.py:310
  24.9 6.4 %copy-start.1 = (bf16[512,512]{1,0:T(8,128)(2,1)S(1)}, bf16[512,512]{1,0:T(8,128)(2,1)}, u32[]{:S(2)}) copy-start(bf16[512,512]{1,0:T(8,128)(2,1)} %weight.17) | copy-start | bytes 1572868
  31.2 1.6 %collective-permute-start.7 = (bf16[256,512]{1,0:T(8,128)(2,1)S(1)}, bf16[256,512]{1,0:T(8,128)(2,1)S(1)}, u32[]{:S(2)}, u32[]{:S(2)}) collective-permute-start(bf16[256,512]{1,0:T(8,128)(2,1)S(1)} %get-tuple-element.59), channel_id=1, source_target_pairs={{0,1},{1,0},{2,3},{3,2},{4,5},{5,4},{6,7},{7,6},{8,9},{9,8},{10,11... | collective-permute-start | bytes 786440 | tf_op jit(solution)/shard_map/ppermute | solution.py:373
  32.9 8.7 %collective-permute-start.8 = (bf16[256,512]{1,0:T(8,128)(2,1)S(1)}, bf16[256,512]{1,0:T(8,128)(2,1)S(1)}, u32[]{:S(2)}, u32[]{:S(2)}) collective-permute-start(bf16[256,512]{1,0:T(8,128)(2,1)S(1)} %add_convert_fusion), channel_id=1, source_target_pairs={{0,2},{1,3},{2,0},{3,1},{4,6},{5,7},{6,4},{7,5},{8,10},{9,11},{10,... | collective-permute-start | bytes 786440 | tf_op jit(solution)/shard_map/ppermute | solution.py:379
  35.0 7.8 %collective-permute-start.9 = (bf16[256,512]{1,0:T(8,128)(2,1)S(1)}, bf16[256,512]{1,0:T(8,128)(2,1)S(1)}, u32[]{:S(2)}, u32[]{:S(2)}) collective-permute-start(bf16[256,512]{1,0:T(8,128)(2,1)S(1)} %add_convert_fusion), channel_id=1, source_target_pairs={{0,1},{1,0},{2,3},{3,2},{4,5},{5,4},{6,7},{7,6},{8,9},{9,8},{10,11... | collective-permute-start | bytes 786440 | tf_op jit(solution)/shard_map/ppermute | solution.py:382
  41.6 1.5 %collective-permute-start.10 = (bf16[256,512]{1,0:T(8,128)(2,1)S(1)}, bf16[256,512]{1,0:T(8,128)(2,1)S(1)}, u32[]{:S(2)}, u32[]{:S(2)}) collective-permute-start(bf16[256,512]{1,0:T(8,128)(2,1)S(1)} %collective-permute-done.8), channel_id=1, source_target_pairs={{0,1},{1,0},{2,3},{3,2},{4,5},{5,4},{6,7},{7,6},{8,9},{9,8},{10,11... | collective-permute-start | bytes 786440 | tf_op jit(solution)/shard_map/ppermute | solution.py:382
where the time goes:
time: 44.5 us; the launch traced here: 44.3 us
  waiting for transfers between devices  17.3 us (39%)
  starting transfers between devices  11.4 us (26%)
  Pallas kernels  11.3 us (25%)
  local copies, waits for them, and re-layouts  1.7 us (4%)
  between operations  1.35 us (3%)
  other arithmetic  1.27 us (3%)
    ppermute x4, waiting for transfers between devices, gathered(): fore = lax.ppermute(fore, 'dp', ahead)  9.36 us
    ppermute x4, starting transfers between devices, gathered(): fore = lax.ppermute(fore, 'dp', ahead)  8.77 us
    ppermute x1, waiting for transfers between devices, gathered(): got = lax.ppermute(sent, 'group', [(i, i ^ move) for i in range(groups)])  6.6 us
    pallas_call x1, Pallas kernels, gathered(): pl.pallas_call(functools.partial(main_kernel, count), out_shape=(pltpu.VM...  6.27 us
    pallas_call x8, Pallas kernels, gathered(): pl.pallas_call(functools.partial(embed_kernel, count, step), out_shape=he...  3.05 us
    ppermute x1, starting transfers between devices, gathered(): got = lax.ppermute(sent, 'group', [(i, i ^ move) for i in range(groups)])  2.06 us
    unnamed x5, local copies, waits for them, and re-layouts  1.7 us
    concatenate x1, other arithmetic, gathered(): return (grad_rows, jnp.concatenate([low, high]), loss.reshape(1))  1.04 us
  transfers between devices with their start and end apart: 11, of which 7 were waited for; matrix products, arithmetic and copies ran while one was open for 1% of the time, Pallas kernels for 8%

commit v1 on v0

--- a/solution.py
+++ b/solution.py
@@ -173,76 +173,87 @@
     return jnp.where(2 * at < count, 2 * at, 2 * (count - 1 - at) + 1)
 
 
-def main_kernel(count, embeds, turned, codes, give, grads, loss, hot_s, g_high, g_low):
+def main_kernel(count, embeds, turned, codes, give, grads, loss, cross, lefts, rights):
     total = embeds.shape[0]
     rows = total // count
-    classes = count * WAYS_MAX
+    slots = WAYS_MAX + -WAYS_MAX % 8
+    classes = count * slots
     scale = D ** (-0.5)
     me = lax.axis_index("dp")
     step = min(total, 256)
     parts = [slice(at, at + step) for at in range(0, total, step)]
+    stretch = [slice(k * classes, (k + 1) * classes) for k in range(4)]
 
     owner, slot, query = codes[0:1, :], codes[1:2, :], codes[2:3, :]
+    members = [owner == float(p) for p in range(count)]
     ways = jnp.zeros_like(owner)
     queries = jnp.zeros_like(owner)
-    for p in range(count):
-        mine = owner == float(p)
+    for p, mine in enumerate(members):
         ways = jnp.where(mine, codes[3:4, p * rows : p * rows + 1], ways)
         total_q = jnp.sum(jnp.where(mine, query, 0.0), axis=1, keepdims=True)
         queries = jnp.where(mine, total_q, queries)
     share = query / jnp.maximum(queries, 1.0)
     label = slot - jnp.floor((slot + 0.5) / ways) * ways
-    first = (owner * float(WAYS_MAX)).astype(jnp.int32)
-    last = first + ways.astype(jnp.int32)
-    own_class = first + label.astype(jnp.int32)
-    support_class = jnp.where(query > 0.5, -1, own_class)
-
-    ids = lax.broadcasted_iota(jnp.int32, (classes, total), 0)
-    hot_value = jnp.where(ids == support_class, 1.0, 0.0)
-    counts = jnp.maximum(jnp.sum(hot_value, axis=1, keepdims=True), 1.0)
-    hot_s[...] = hot_value.astype(jnp.bfloat16)
-    protos = dot(hot_s[...], embeds[...]) / counts
+    line = lax.broadcasted_iota(jnp.int32, (16, total), 0).astype(jnp.float32)
+    by_owner = jnp.where(line == owner, 1.0, 0.0).astype(jnp.bfloat16)
+
+    def spread(value, *places):
+        for p in range(0, count, 2):
+            pair = jnp.concatenate([jnp.where(mine, value, 0.0) for mine in members[p : p + 2]])
+            pair = pair.astype(jnp.bfloat16)
+            for k in places:
+                at = k * classes + p * slots
+                lefts[at : at + pair.shape[0], :] = pair
+
+    def column(table):
+        return jnp.concatenate([table[:, p : p + 1] for p in range(count)])
+
+    ids = lax.broadcasted_iota(jnp.int32, (slots, total), 0).astype(jnp.float32)
+    is_own = ids == label
+    own_value = jnp.where(is_own, 1.0, 0.0)
+    hot_value = jnp.where(query > 0.5, 0.0, own_value)
+    spread(hot_value, 3)
+    counts = dot(hot_value.astype(jnp.bfloat16), by_owner, (1, 1))
+    per_class = column(1.0 / jnp.maximum(counts, 1.0))
+    protos = dot(lefts[stretch[3], :], embeds[...]) * per_class
     p_high, p_low = split(protos)
-    p_length = jnp.sum(protos * protos, axis=1, keepdims=True)
-
-    g_sum = jnp.zeros((classes, 1), jnp.float32)
-    loss_sum = jnp.zeros((1, 1), jnp.float32)
-    row_sums = []
+    rights[stretch[0], :] = p_high
+    rights[stretch[1], :] = p_high
+    rights[stretch[2], :] = p_low
+    half_length = 0.5 * jnp.sum(protos * protos, axis=1, keepdims=True)
+
     for part in parts:
         e = embeds[part, :]
-        product = dot(p_high, e, (1, 1)) + dot(p_low, e, (1, 1))
-        scores = -(codes[4:5, part] - 2.0 * product + p_length) * scale
-        c = lax.broadcasted_iota(jnp.int32, (classes, step), 0)
-        masked = jnp.where((c >= first[:, part]) & (c < last[:, part]), scores, -1e30)
-        top = jnp.max(masked, axis=0, keepdims=True)
-        powers = jnp.exp(masked - top)
-        norm = jnp.sum(powers, axis=0, keepdims=True)
-        is_own = c == own_class[:, part]
-        picked = jnp.sum(jnp.where(is_own, scores, 0.0), axis=0, keepdims=True)
-        mine = owner[:, part] == me.astype(jnp.float32)
-        losses = share[:, part] * (top + jnp.log(norm) - picked)
-        loss_sum += jnp.sum(jnp.where(mine, losses, 0.0), axis=1, keepdims=True)
-        g = (powers * (1.0 / norm) - jnp.where(is_own, 1.0, 0.0)) * (
-            share[:, part] * (2.0 * scale)
-        )
-        g_sum += jnp.sum(g, axis=1, keepdims=True)
-        row_sums.append(jnp.sum(g, axis=0, keepdims=True))
-        high, low = split(g)
-        g_high[:, part] = high
-        g_low[:, part] = low
-    loss[...] = jnp.broadcast_to(loss_sum, loss.shape)
+        product = dot(rights[classes : 3 * classes, :], e, (1, 1))
+        product = product[:classes, :] + product[classes:, :] - half_length
+        picked = jnp.zeros((slots, step), jnp.float32)
+        for p, mine in enumerate(members):
+            picked = jnp.where(mine[:, part], product[p * slots : (p + 1) * slots, :], picked)
+        cross[:, part] = picked
+    scores = (2.0 * cross[...] - codes[4:5, :]) * scale
+    masked = jnp.where(ids < ways, scores, -1e30)
+    top = jnp.max(masked, axis=0, keepdims=True)
+    powers = jnp.exp(masked - top)
+    norm = jnp.sum(powers, axis=0, keepdims=True)
+    picked = jnp.sum(jnp.where(is_own, scores, 0.0), axis=0, keepdims=True)
+    losses = share * (top + jnp.log(norm) - picked)
+    losses = jnp.where(owner == me.astype(jnp.float32), losses, 0.0)
+    loss[...] = jnp.broadcast_to(jnp.sum(losses, axis=1, keepdims=True), loss.shape)
+    g = (powers * (1.0 / norm) - own_value) * (share * (2.0 * scale))
+    row_sum = jnp.sum(g, axis=0, keepdims=True)
+    high, low = split(g)
+    spread(high.astype(jnp.float32), 1, 2)
+    spread(low.astype(jnp.float32), 0)
+    g_sum = column(dot(high, by_owner, (1, 1)) + dot(low, by_owner, (1, 1)))
 
     e = embeds[...]
-    d_protos = dot(g_high[...], e) + dot(g_low[...], e) - g_sum * protos
-    s_high = (d_protos / counts).astype(jnp.bfloat16)
-    for part, row_sum in zip(parts, row_sums):
-        value = (
-            dot(g_high[:, part], p_high, (0, 0))
-            + dot(g_low[:, part], p_high, (0, 0))
-            + dot(g_high[:, part], p_low, (0, 0))
-            + dot(hot_s[:, part], s_high, (0, 0))
-        )
-        back = jnp.broadcast_to(row_sum, (128, step)).T[:, :1]
+    d_protos = dot(lefts[: 2 * classes, :], e)
+    d_protos = d_protos[classes:, :] + d_protos[:classes, :] - g_sum * protos
+    rights[stretch[3], :] = (d_protos * per_class).astype(jnp.bfloat16)
+    wide = min(total, 512)
+    for part in [slice(at, at + wide) for at in range(0, total, wide)]:
+        value = dot(lefts[:, part], rights[...], (0, 0))
+        back = jnp.broadcast_to(row_sum[:, part], (128, wide)).T[:, :1]
         value = value - back * embeds[part, :].astype(jnp.float32)
         grads[part, :] = value.astype(jnp.bfloat16)
 
@@ -272,7 +283,7 @@
     count = lax.axis_size("dp")
     groups = lax.axis_size("group")
     rows = features.shape[0]
-    classes = count * WAYS_MAX
+    slots = WAYS_MAX + -WAYS_MAX % 8
     total = rows * count
 
     order = ring_order(count)
@@ -342,7 +353,11 @@
         ),
         in_specs=vmem(3),
         out_specs=tuple(vmem(3)),
-        scratch_shapes=[pltpu.VMEM((classes, total), jnp.bfloat16)] * 3,
+        scratch_shapes=[
+            pltpu.VMEM((slots, total), jnp.float32),
+            pltpu.VMEM((4 * count * slots, total), jnp.bfloat16),
+            pltpu.VMEM((4 * count * slots, D), jnp.bfloat16),
+        ],
         compiler_params=pltpu.CompilerParams(vmem_limit_bytes=32 * 2**20),
         name="episodes",
     )(*state)

time: 44.5 us -> 43.5 us (0.978)
  Pallas kernels: 11.3 us -> 10.3 us
    pallas_call x1, Pallas kernels: 6.27 us -> 5.28 us  [gathered(): pl.pallas_call(functools.partial(main_kernel, count), out_shape=(pltpu.VM...]
  transfers between devices with their start and end apart: 11 -> 11, of which waited for: 7 -> 7; matrix products, arithmetic and copies ran while one was open for 1% -> 2% of each run, Pallas kernels for 8% -> 9%
where the time goes in v1:
time: 43.5 us; the launch traced here: 43.3 us
  waiting for transfers between devices  17.3 us (40%)
  starting transfers between devices  11.4 us (26%)
  Pallas kernels  10.3 us (24%)
  local copies, waits for them, and re-layouts  1.7 us (4%)
  between operations  1.35 us (3%)
  other arithmetic  1.27 us (3%)
    ppermute x4, waiting for transfers between devices, gathered(): fore = lax.ppermute(fore, 'dp', ahead)  9.36 us
    ppermute x4, starting transfers between devices, gathered(): fore = lax.ppermute(fore, 'dp', ahead)  8.77 us
    ppermute x1, waiting for transfers between devices, gathered(): got = lax.ppermute(sent, 'group', [(i, i ^ move) for i in range(groups)])  6.6 us
    pallas_call x1, Pallas kernels, gathered(): pl.pallas_call(functools.partial(main_kernel, count), out_shape=(pltpu.VM...  5.28 us
    pallas_call x8, Pallas kernels, gathered(): pl.pallas_call(functools.partial(embed_kernel, count, step), out_shape=he...  3.05 us
    ppermute x1, starting transfers between devices, gathered(): got = lax.ppermute(sent, 'group', [(i, i ^ move) for i in range(groups)])  2.05 us
    unnamed x5, local copies, waits for them, and re-layouts  1.7 us
    concatenate x1, other arithmetic, gathered(): return (grad_rows, jnp.concatenate([low, high]), loss.reshape(1))  1.04 us
  transfers between devices with their start and end apart: 11, of which 7 were waited for; matrix products, arithmetic and copies ran while one was open for 2% of the time, Pallas kernels for 9%

profile of v1, /device:TPU:0, one launch (start us, length us, event | category | flops | bytes accessed | tf_op | source)
XLA Modules:
  0.0 43.3 jit_solution(16154285840699022788)
XLA Ops:
  1.3 0.9 %pack.1.block = bf16[136,512]{1,0:T(8,128)(2,1)S(1)} custom-call(bf16[128,512]{1,0:T(8,128)(2,1)} %features.1, s32[1,128]{1,0:T(1,128)} %bitcast.6, s32[1,128]{1,0:T(1,128)} %bitcast.7, s32[1,128]{1,0:T(1,128)} %bitcast.8, s32[1,1]{1,0:T(1,128)} %bitcast.5.ways), custom_call_target="tpu_custom_call" | custom-call | tf_op jit(solution)/shard_map/pack/pallas_call | solution.py:294
  2.2 3.1 %collective-permute-start = (bf16[136,512]{1,0:T(8,128)(2,1)S(1)}, bf16[136,512]{1,0:T(8,128)(2,1)S(1)}, u32[]{:S(2)}, u32[]{:S(2)}) collective-permute-start(bf16[136,512]{1,0:T(8,128)(2,1)S(1)} %pack.1.block), channel_id=1, source_target_pairs={{0,8},{8,16},{16,24},{24,28},{28,20},{20,12},{12,4},{4,0},{1,9},{9... | collective-permute-start | bytes 417800 | tf_op jit(solution)/shard_map/ppermute | solution.py:321
  5.3 1.0 %copy-done = bf16[512,512]{1,0:T(8,128)(2,1)S(1)} copy-done((bf16[512,512]{1,0:T(8,128)(2,1)S(1)}, bf16[512,512]{1,0:T(8,128)(2,1)}, u32[]{:S(2)}) %copy-start) | copy-done | bytes 524312
  6.4 0.4 embed.8
  6.8 2.2 %collective-permute-done.block = bf16[136,512]{1,0:T(8,128)(2,1)S(1)} collective-permute-done((bf16[136,512]{1,0:T(8,128)(2,1)S(1)}, bf16[136,512]{1,0:T(8,128)(2,1)S(1)}, u32[]{:S(2)}, u32[]{:S(2)}) %collective-permute-start) | collective-permute-done | bytes 139296 | tf_op jit(solution)/shard_map/ppermute | solution.py:321
  8.9 1.8 %collective-permute-start.1 = (bf16[136,512]{1,0:T(8,128)(2,1)S(1)}, bf16[136,512]{1,0:T(8,128)(2,1)S(1)}, u32[]{:S(2)}, u32[]{:S(2)}) collective-permute-start(bf16[136,512]{1,0:T(8,128)(2,1)S(1)} %collective-permute-done.block), channel_id=1, source_target_pairs={{0,8},{8,16},{16,24},{24,28},{28,20},{20,12},{12,4},{4,0},{1,9},{9... | collective-permute-start | bytes 417800 | tf_op jit(solution)/shard_map/ppermute | solution.py:321
  10.7 0.2 collective-permute-start.5
  11.0 0.4 embed.9
  11.4 0.4 embed.10
  11.7 2.3 %collective-permute-done.1.block = bf16[136,512]{1,0:T(8,128)(2,1)S(1)} collective-permute-done((bf16[136,512]{1,0:T(8,128)(2,1)S(1)}, bf16[136,512]{1,0:T(8,128)(2,1)S(1)}, u32[]{:S(2)}, u32[]{:S(2)}) %collective-permute-start.1) | collective-permute-done | bytes 139296 | tf_op jit(solution)/shard_map/ppermute | solution.py:321
  14.0 1.8 %collective-permute-start.2 = (bf16[136,512]{1,0:T(8,128)(2,1)S(1)}, bf16[136,512]{1,0:T(8,128)(2,1)S(1)}, u32[]{:S(2)}, u32[]{:S(2)}) collective-permute-start(bf16[136,512]{1,0:T(8,128)(2,1)S(1)} %collective-permute-done.1.block), channel_id=1, source_target_pairs={{0,8},{8,16},{16,24},{24,28},{28,20},{20,12},{12,4},{4,0},{1,9},{9... | collective-permute-start | bytes 417800 | tf_op jit(solution)/shard_map/ppermute | solution.py:321
  15.8 0.2 collective-permute-start.6
  16.0 0.4 embed.11
  16.4 0.4 embed.12
  16.8 2.7 %collective-permute-done.2.block = bf16[136,512]{1,0:T(8,128)(2,1)S(1)} collective-permute-done((bf16[136,512]{1,0:T(8,128)(2,1)S(1)}, bf16[136,512]{1,0:T(8,128)(2,1)S(1)}, u32[]{:S(2)}, u32[]{:S(2)}) %collective-permute-start.2) | collective-permute-done | bytes 139296 | tf_op jit(solution)/shard_map/ppermute | solution.py:321
  19.5 2.1 %collective-permute-start.3 = (bf16[136,512]{1,0:T(8,128)(2,1)S(1)}, bf16[136,512]{1,0:T(8,128)(2,1)S(1)}, u32[]{:S(2)}, u32[]{:S(2)}) collective-permute-start(bf16[136,512]{1,0:T(8,128)(2,1)S(1)} %collective-permute-done.2.block), channel_id=1, source_target_pairs={{0,8},{8,16},{16,24},{24,28},{28,20},{20,12},{12,4},{4,0},{1,9},{9... | collective-permute-start | bytes 417800 | tf_op jit(solution)/shard_map/ppermute | solution.py:321
  21.6 0.4 embed.13
  22.0 0.4 embed.14
  22.4 2.2 %collective-permute-done.3.block = bf16[136,512]{1,0:T(8,128)(2,1)S(1)} collective-permute-done((bf16[136,512]{1,0:T(8,128)(2,1)S(1)}, bf16[136,512]{1,0:T(8,128)(2,1)S(1)}, u32[]{:S(2)}, u32[]{:S(2)}) %collective-permute-start.3) | collective-permute-done | bytes 139296 | tf_op jit(solution)/shard_map/ppermute | solution.py:321
  24.6 0.4 embed.15
  24.9 5.3 %episodes.1 = (bf16[256,512]{1,0:T(8,128)(2,1)S(1)}, bf16[1024,512]{1,0:T(8,128)(2,1)S(1)}, f32[8,128]{1,0:T(8,128)S(1)}) custom-call(bf16[1024,512]{1,0:T(8,128)(2,1)S(1)} %get-tuple-element.54.embeds, bf16[512,1024]{1,0:T(8,128)(2,1)S(1)} %get-tuple-element.53.turned, f32[8,1024]{1,0:T(8,128)S(1)} %get-tuple-element.55.codes), custom_call_target="tpu_custom_call" | custom-call | tf_op jit(solution)/shard_map/episodes/pallas_call | solution.py:347
  30.2 0.1 collective-permute-start.7
  30.3 0.5 %rest.1 = (f32[256,512]{1,0:T(8,128)S(1)}, bf16[128,512]{1,0:T(8,128)(2,1)S(1)}) custom-call(bf16[512,1024]{1,0:T(8,128)(2,1)S(1)} %get-tuple-element.53.turned, bf16[1024,512]{1,0:T(8,128)(2,1)S(1)} %get-tuple-element.56.grads, bf16[512,512]{1,0:T(8,128)(2,1)S(1)} %copy-done.1), custom_call_target="tpu_custom_call" | custom-call | flops 4294967296 | tf_op jit(solution)/shard_map/rest/pallas_call | solution.py:364
  30.9 1.0 %collective-permute-done.7 = bf16[256,512]{1,0:T(8,128)(2,1)S(1)} collective-permute-done((bf16[256,512]{1,0:T(8,128)(2,1)S(1)}, bf16[256,512]{1,0:T(8,128)(2,1)S(1)}, u32[]{:S(2)}, u32[]{:S(2)}) %collective-permute-start.7) | collective-permute-done | bytes 262176 | tf_op jit(solution)/shard_map/ppermute | solution.py:388
  31.8 0.1 add_convert_fusion
  31.9 2.1 %collective-permute-start.8 = (bf16[256,512]{1,0:T(8,128)(2,1)S(1)}, bf16[256,512]{1,0:T(8,128)(2,1)S(1)}, u32[]{:S(2)}, u32[]{:S(2)}) collective-permute-start(bf16[256,512]{1,0:T(8,128)(2,1)S(1)} %add_convert_fusion), channel_id=1, source_target_pairs={{0,2},{1,3},{2,0},{3,1},{4,6},{5,7},{6,4},{7,5},{8,10},{9,11},{10,... | collective-permute-start | bytes 786440 | tf_op jit(solution)/shard_map/ppermute | solution.py:394
  34.0 6.6 %collective-permute-done.8 = bf16[256,512]{1,0:T(8,128)(2,1)S(1)} collective-permute-done((bf16[256,512]{1,0:T(8,128)(2,1)S(1)}, bf16[256,512]{1,0:T(8,128)(2,1)S(1)}, u32[]{:S(2)}, u32[]{:S(2)}) %collective-permute-start.8) | collective-permute-done | bytes 262176 | tf_op jit(solution)/shard_map/ppermute | solution.py:394
  40.6 0.7 %copy.51 = bf16[128,512]{1,0:T(8,128)(2,1)} copy(bf16[128,512]{1,0:T(8,128)(2,1)S(1)} %get-tuple-element.63) | data formatting | bytes 262144
  41.2 0.5 %loss.1 = f32[1,1]{1,0:T(1,128)} custom-call(f32[8,128]{1,0:T(8,128)S(1)} %get-tuple-element.60.value), custom_call_target="tpu_custom_call" | custom-call | flops 268435456 | tf_op jit(solution)/shard_map/loss/pallas_call | solution.py:377
  41.7 0.4 collective-permute-done.10
  42.1 0.2 fusion.1
  42.3 1.0 %pad_maximum_fusion = f32[512,512]{1,0:T(8,128)} fusion(f32[256,512]{1,0:T(8,128)S(1)} %get-tuple-element.62, f32[256,512]{1,0:T(8,128)S(1)} %get-tuple-element.61), kind=kLoop, calls=%fused_computation | loop fusion | flops 262144 | bytes 2097152 | tf_op jit(solution)/shard_map/concatenate | solution.py:403
  (10 shorter events, 0.0 us)
Async XLA Ops:
  2.2 6.7 %collective-permute-start = (bf16[136,512]{1,0:T(8,128)(2,1)S(1)}, bf16[136,512]{1,0:T(8,128)(2,1)S(1)}, u32[]{:S(2)}, u32[]{:S(2)}) collective-permute-start(bf16[136,512]{1,0:T(8,128)(2,1)S(1)} %pack.1.block), channel_id=1, source_target_pairs={{0,8},{8,16},{16,24},{24,28},{28,20},{20,12},{12,4},{4,0},{1,9},{9... | collective-permute-start | bytes 417800 | tf_op jit(solution)/shard_map/ppermute | solution.py:321
  5.3 5.4 %collective-permute-start.4 = (bf16[136,512]{1,0:T(8,128)(2,1)S(1)}, bf16[136,512]{1,0:T(8,128)(2,1)S(1)}, u32[]{:S(2)}, u32[]{:S(2)}) collective-permute-start(bf16[136,512]{1,0:T(8,128)(2,1)S(1)} %pack.1.block), channel_id=1, source_target_pairs={{8,0},{16,8},{24,16},{28,24},{20,28},{12,20},{4,12},{0,4},{9,1},{1... | collective-permute-start | bytes 417800 | tf_op jit(solution)/shard_map/ppermute | solution.py:324
  5.3 1.0 %copy-start = (bf16[512,512]{1,0:T(8,128)(2,1)S(1)}, bf16[512,512]{1,0:T(8,128)(2,1)}, u32[]{:S(2)}) copy-start(bf16[512,512]{1,0:T(8,128)(2,1)} %weight.17) | copy-start | bytes 1572868
  8.9 5.1 %collective-permute-start.1 = (bf16[136,512]{1,0:T(8,128)(2,1)S(1)}, bf16[136,512]{1,0:T(8,128)(2,1)S(1)}, u32[]{:S(2)}, u32[]{:S(2)}) collective-permute-start(bf16[136,512]{1,0:T(8,128)(2,1)S(1)} %collective-permute-done.block), channel_id=1, source_target_pairs={{0,8},{8,16},{16,24},{24,28},{28,20},{20,12},{12,4},{4,0},{1,9},{9... | collective-permute-start | bytes 417800 | tf_op jit(solution)/shard_map/ppermute | solution.py:321
  10.7 5.1 %collective-permute-start.5 = (bf16[136,512]{1,0:T(8,128)(2,1)S(1)}, bf16[136,512]{1,0:T(8,128)(2,1)S(1)}, u32[]{:S(2)}, u32[]{:S(2)}) collective-permute-start(bf16[136,512]{1,0:T(8,128)(2,1)S(1)} %collective-permute-done.4.block), channel_id=1, source_target_pairs={{8,0},{16,8},{24,16},{28,24},{20,28},{12,20},{4,12},{0,4},{9,1},{1... | collective-permute-start | bytes 417800 | tf_op jit(solution)/shard_map/ppermute | solution.py:324
  14.0 5.5 %collective-permute-start.2 = (bf16[136,512]{1,0:T(8,128)(2,1)S(1)}, bf16[136,512]{1,0:T(8,128)(2,1)S(1)}, u32[]{:S(2)}, u32[]{:S(2)}) collective-permute-start(bf16[136,512]{1,0:T(8,128)(2,1)S(1)} %collective-permute-done.1.block), channel_id=1, source_target_pairs={{0,8},{8,16},{16,24},{24,28},{28,20},{20,12},{12,4},{4,0},{1,9},{9... | collective-permute-start | bytes 417800 | tf_op jit(solution)/shard_map/ppermute | solution.py:321
  15.8 6.2 %collective-permute-start.6 = (bf16[136,512]{1,0:T(8,128)(2,1)S(1)}, bf16[136,512]{1,0:T(8,128)(2,1)S(1)}, u32[]{:S(2)}, u32[]{:S(2)}) collective-permute-start(bf16[136,512]{1,0:T(8,128)(2,1)S(1)} %collective-permute-done.5.block), channel_id=1, source_target_pairs={{8,0},{16,8},{24,16},{28,24},{20,28},{12,20},{4,12},{0,4},{9,1},{1... | collective-permute-start | bytes 417800 | tf_op jit(solution)/shard_map/ppermute | solution.py:324
  19.5 5.1 %collective-permute-start.3 = (bf16[136,512]{1,0:T(8,128)(2,1)S(1)}, bf16[136,512]{1,0:T(8,128)(2,1)S(1)}, u32[]{:S(2)}, u32[]{:S(2)}) collective-permute-start(bf16[136,512]{1,0:T(8,128)(2,1)S(1)} %collective-permute-done.2.block), channel_id=1, source_target_pairs={{0,8},{8,16},{16,24},{24,28},{28,20},{20,12},{12,4},{4,0},{1,9},{9... | collective-permute-start | bytes 417800 | tf_op jit(solution)/shard_map/ppermute | solution.py:321
  24.9 5.4 %copy-start.1 = (bf16[512,512]{1,0:T(8,128)(2,1)S(1)}, bf16[512,512]{1,0:T(8,128)(2,1)}, u32[]{:S(2)}) copy-start(bf16[512,512]{1,0:T(8,128)(2,1)} %weight.17) | copy-start | bytes 1572868
  30.2 1.6 %collective-permute-start.7 = (bf16[256,512]{1,0:T(8,128)(2,1)S(1)}, bf16[256,512]{1,0:T(8,128)(2,1)S(1)}, u32[]{:S(2)}, u32[]{:S(2)}) collective-permute-start(bf16[256,512]{1,0:T(8,128)(2,1)S(1)} %get-tuple-element.59), channel_id=1, source_target_pairs={{0,1},{1,0},{2,3},{3,2},{4,5},{5,4},{6,7},{7,6},{8,9},{9,8},{10,11... | collective-permute-start | bytes 786440 | tf_op jit(solution)/shard_map/ppermute | solution.py:388
  31.9 8.7 %collective-permute-start.8 = (bf16[256,512]{1,0:T(8,128)(2,1)S(1)}, bf16[256,512]{1,0:T(8,128)(2,1)S(1)}, u32[]{:S(2)}, u32[]{:S(2)}) collective-permute-start(bf16[256,512]{1,0:T(8,128)(2,1)S(1)} %add_convert_fusion), channel_id=1, source_target_pairs={{0,2},{1,3},{2,0},{3,1},{4,6},{5,7},{6,4},{7,5},{8,10},{9,11},{10,... | collective-permute-start | bytes 786440 | tf_op jit(solution)/shard_map/ppermute | solution.py:394
  34.0 7.8 %collective-permute-start.9 = (bf16[256,512]{1,0:T(8,128)(2,1)S(1)}, bf16[256,512]{1,0:T(8,128)(2,1)S(1)}, u32[]{:S(2)}, u32[]{:S(2)}) collective-permute-start(bf16[256,512]{1,0:T(8,128)(2,1)S(1)} %add_convert_fusion), channel_id=1, source_target_pairs={{0,1},{1,0},{2,3},{3,2},{4,5},{5,4},{6,7},{7,6},{8,9},{9,8},{10,11... | collective-permute-start | bytes 786440 | tf_op jit(solution)/shard_map/ppermute | solution.py:397
  40.6 1.5 %collective-permute-start.10 = (bf16[256,512]{1,0:T(8,128)(2,1)S(1)}, bf16[256,512]{1,0:T(8,128)(2,1)S(1)}, u32[]{:S(2)}, u32[]{:S(2)}) collective-permute-start(bf16[256,512]{1,0:T(8,128)(2,1)S(1)} %collective-permute-done.8), channel_id=1, source_target_pairs={{0,1},{1,0},{2,3},{3,2},{4,5},{5,4},{6,7},{7,6},{8,9},{9,8},{10,11... | collective-permute-start | bytes 786440 | tf_op jit(solution)/shard_map/ppermute | solution.py:397
